TPU v7x, 32 devices: a whole 2x2x4 slice. The times are simulated.
32 devices in a mesh: replica: 16 (over z, y, core), model: 2 (over x).
Axes of the slice: x: 2, y: 2, z: 4, core: 2. Of those that a mesh axis runs over, the one named last changes fastest.
Arguments:
- layer_grads: bfloat16 [16, 2, 4096, 1024], P('replica', None, 'model'), may hold values from -6 to 6
- last_basis: float32 [2, 1024, 32], replicated, may hold values from -6 to 6
- layer_weights: float32 [2, 4096, 1024], P(None, 'model', 'replica'), may hold values from -0.1875 to 0.1875
- momentum: float32 [2, 4096, 1024], P(None, 'model', 'replica'), may hold values from -0.3125 to 0.3125
Outputs:
- new_weights: float32 [2, 4096, 1024], P(None, 'model', 'replica')
- new_basis: float32 [2, 1024, 32], replicated
- new_momentum: float32 [2, 4096, 1024], P(None, 'model', 'replica')
All inputs are finite; a program needn't handle non-finite values.
Results may differ from a plain program's by a relative error of at most 0.0029.
Values sent between devices are 32-bit elements; how exact they have to be, the bound alone decides.
A program may use at most 64 MiB of HBM per device.

v0:
```python
import jax
import jax.numpy as jnp
from jax import lax
from jax.sharding import PartitionSpec as P

RANK = 32


def shards(layer_grads, last_basis, layer_weights, momentum):
    own_grads = layer_grads[0]
    part_left = jnp.einsum(
        "liw,lwr->lir",
        own_grads,
        last_basis.astype(jnp.bfloat16),
        preferred_element_type=jnp.float32,
    )
    shares = lax.psum_scatter(part_left, "replica", scatter_dimension=1, tiled=True)
    left = lax.all_gather(shares, "replica", axis=1, tiled=True)
    part_gram = jnp.einsum("lir,lis->lrs", left, left, precision=lax.Precision.HIGHEST)
    small_left = left.astype(jnp.bfloat16)
    gram = lax.psum(part_gram, "model")
    part_right = jnp.einsum(
        "liw,lir->lwr", own_grads, small_left, preferred_element_type=jnp.float32
    )
    right = lax.psum(part_right, ("replica", "model"))
    gram = gram + 0.001 * jnp.mean(jnp.diagonal(gram, axis1=1, axis2=2), axis=1)[
        :, None, None
    ] * jnp.eye(RANK, dtype=jnp.float32)
    place = lax.axis_index("replica") * layer_weights.shape[2]
    own_right = lax.dynamic_slice_in_dim(right, place, layer_weights.shape[2], axis=1)
    root = jnp.linalg.cholesky(gram)
    half = lax.linalg.triangular_solve(
        root, jnp.swapaxes(own_right, 1, 2), left_side=True, lower=True
    )
    mixed = lax.linalg.triangular_solve(root, half, left_side=True, lower=True, transpose_a=True)
    change = jnp.einsum(
        "lir,lrw->liw", left, mixed, precision=lax.Precision.HIGHEST
    ) / lax.axis_size("replica")
    new_momentum = 0.9 * momentum + change
    new_weights = layer_weights - 0.02 * new_momentum
    new_basis = right * lax.rsqrt(jnp.mean(right * right, axis=(1, 2), keepdims=True) + 1e-12)
    return (new_weights, new_basis, new_momentum)


def solution(mesh):
    in_specs = (
        P("replica", None, "model", None),
        P(),
        P(None, "model", "replica"),
        P(None, "model", "replica"),
    )
    out_specs = (P(None, "model", "replica"), P(), P(None, "model", "replica"))
    return jax.shard_map(shards, mesh=mesh, in_specs=in_specs, out_specs=out_specs, check_vma=False)
```

profile of v0, /device:TPU:0, one launch (start us, length us, event | category | flops | bytes accessed | tf_op | source)
XLA Modules:
  0.0 245.5 jit_solution(10136461796317535133)
XLA Ops:
  7.2 0.0 reduce-scatter.2.cloned.1.call-start
  7.2 6.7 %fusion.2 = f32[2,2048,32]{1,2,0:T(8,128)} fusion(bf16[1,2,2048,1024]{3,2,1,0:T(8,128)(2,1)} %param.4, f32[2,1024,32]{1,2,0:T(8,128)} %param.5), kind=kOutput, calls=%fused_computation.3 | convolution fusion | flops 268500992 | bytes 9175040 | tf_op jit(solution)/shard_map/liw,lwr->lir/dot_general | solution.py:11
  14.0 0.0 all-reduce.2.cloned.1.call-start
  14.0 0.1 copy.13
  14.2 58.9 %reduce-scatter.2.cloned.1.call-done = f32[2,128,32]{1,2,0:T(8,128)} async-done(((f32[2,2048,32]{1,2,0:T(8,128)}), f32[2,128,32]{1,2,0:T(8,128)}) %reduce-scatter.2.cloned.1.call-update) | async-done | bytes 32784 | tf_op jit(solution)/shard_map/reduce_scatter | solution.py:17
  73.1 21.1 %all_gather.3 = f32[2,2048,32]{1,2,0:T(8,128)S(1)} all-gather(f32[2,128,32]{1,2,0:T(8,128)} %reduce-scatter.2.cloned.1.call-done), channel_id=1, replica_groups=mesh['replica'=16,'model'=2] {'replica'}, dimensions={1}, use_global_device_ids=true | all-gather | bytes 557056 | tf_op jit(solution)/shard_map/all_gather | solution.py:18
  94.1 0.6 fusion.18
  94.7 5.8 %fusion.5 = f32[2,1024,32]{1,2,0:T(8,128)} fusion(bf16[1,2,2048,1024]{3,2,1,0:T(8,128)(2,1)} %param.4, f32[2,2048,32]{1,2,0:T(8,128)S(1)} %all_gather.3), kind=kOutput, calls=%fused_computation.7 | convolution fusion | flops 268566528 | bytes 9175040 | tf_op jit(solution)/shard_map/liw,lir->lwr/dot_general | solution.py:22
  100.5 8.3 %psum.14 = f32[2,32,32]{1,2,0:T(8,128)S(1)} all-reduce(f32[2,32,32]{1,2,0:T(8,128)S(1)} %fusion.18), channel_id=1, replica_groups=mesh['replica'=16,'model'=2] {'model'}, use_global_device_ids=true, to_apply=%region_1.0 | all-reduce | flops 2048 | bytes 16384 | tf_op jit(solution)/shard_map/psum | solution.py:21
  108.9 0.6 copy.12
  109.4 0.7 gather_fusion
  110.2 0.1 multiply_add_fusion
  110.2 0.1 copy.14
  110.3 0.1 fusion.14
  110.4 5.9 %custom-call.9 = f32[2,32,32]{2,1,0:T(8,128)S(1)} custom-call(f32[2,32,32]{2,1,0:T(8,128)S(1)} %fusion.14), custom_call_target="Cholesky" | custom-call | tf_op jit(solution)/shard_map/jit(cholesky)/cholesky | solution.py:31
  116.3 0.1 compare_reduce_fusion
  116.4 0.1 select_bitcast_fusion
  116.5 4.9 %custom-call.10 = f32[2,1,32,32]{2,3,1,0:T(8,128)S(1)} custom-call(f32[2,1,32,32]{3,2,1,0:T(8,128)S(1)} %select_bitcast_fusion), custom_call_target="InvertDiagBlocksLowerTriangular" | custom-call | tf_op jit(solution)/shard_map/triangular_solve | solution.py:35
  121.4 110.8 %all-reduce.2.cloned.1.call-done = f32[2,1024,32]{1,2,0:T(8,128)} async-done(((f32[2,1024,32]{1,2,0:T(8,128)}), f32[2,1024,32]{1,2,0:T(8,128)}) %all-reduce.2.cloned.1.call-update) | async-done | bytes 262160 | tf_op jit(solution)/shard_map/psum | solution.py:25
  232.1 1.1 multiply_reduce_fusion
  233.2 1.0 fusion.12
  234.3 0.2 fusion.10
  234.4 2.5 %multiply_subtract_fusion = (f32[2,2048,64]{1,2,0:T(8,128)}, f32[2,2048,64]{1,2,0:T(8,128)}) fusion(f32[2,2048,64]{1,2,0:T(8,128)S(1)} %copy-done, f32[2,2048,32]{1,2,0:T(8,128)S(1)} %all_gather.3, f32[2,32,64]{2,1,0:T(8,128)S(1)} %fusion.10, f32[2,2048,64]{1,2,0:T(8,128)S(1)} %copy-done.1), kind=kOutput, calls=%fused_computation.8 | convolution fusion | flops 101974016 | bytes 4734976 | tf_op jit(solution)/shard_map/lir,lrw->liw/dot_general | solution.py:36
  236.9 1.7 broadcast_multiply_fusion
  (14 shorter events, 0.1 us)
Async XLA Ops:
  7.2 65.9 %reduce-scatter.2.cloned.1.call-start = ((), (), s32[]{:S(2)}) async-start(), calls=%async_computation.1 | async-start | bytes 557056 | tf_op jit(solution)/shard_map/reduce_scatter | solution.py:17
  14.0 218.2 %all-reduce.2.cloned.1.call-start = ((), (), s32[]{:S(2)}) async-start(), calls=%async_computation.2 | async-start | bytes 524288 | tf_op jit(solution)/shard_map/psum | solution.py:25
  94.7 139.7 %copy-start = (f32[2,2048,64]{1,2,0:T(8,128)S(1)}, f32[2,2048,64]{1,2,0:T(8,128)}, u32[]{:S(2)}) copy-start(f32[2,2048,64]{1,2,0:T(8,128)} %param.6) | copy-start | bytes 3145732
  94.7 139.7 %copy-start.1 = (f32[2,2048,64]{1,2,0:T(8,128)S(1)}, f32[2,2048,64]{1,2,0:T(8,128)}, u32[]{:S(2)}) copy-start(f32[2,2048,64]{1,2,0:T(8,128)} %param.7) | copy-start | bytes 3145732
Sparse Core Ops, SparseCore 0:
  14.1 58.9 reduce-scatter.1
  109.0 123.1 all-reduce.1
where the time goes:
time: 246 us
  waiting for transfers between devices  170 us (69%)
  blocking collectives  29.4 us (12%)
  matrix products  16.8 us (7%)
  between operations  14.1 us (6%)
  other arithmetic  14 us (6%)
    psum x1, waiting for transfers between devices, shards(): right = lax.psum(part_right, ('replica', 'model'))  111 us
    reduce_scatter x1, waiting for transfers between devices, shards(): lax.psum_scatter(part_left, 'replica', scatter_dimension=1, tiled=True)  58.9 us
    all_gather x1, blocking collectives, shards(): left = lax.all_gather(shares, 'replica', axis=1, tiled=True)  21.1 us
    psum x1, blocking collectives, shards(): gram = lax.psum(part_gram, 'model')  8.32 us
    dot_general x1, matrix products, shards(): jnp.einsum('liw,lwr->lir', own_grads, last_basis.astype(jnp.bfloat16), pr...  6.75 us
    another operation x4, other arithmetic, shards(): root = jnp.linalg.cholesky(gram)  6.01 us
    dot_general x1, matrix products, shards(): jnp.einsum('liw,lir->lwr', own_grads, small_left, preferred_element_type=...  5.78 us
    another operation x3, other arithmetic, shards(): lax.linalg.triangular_solve(root, half, left_side=True, lower=True, trans...  5 us
  transfers between devices with their start and end apart: 2, of which 2 were waited for; matrix products, arithmetic and copies ran while one was open for 5% of the time, Pallas kernels for 0%

commit v1 on v0

--- a/solution.py
+++ b/solution.py
@@ -22,7 +22,7 @@
     part_right = jnp.einsum(
         "liw,lir->lwr", own_grads, small_left, preferred_element_type=jnp.float32
     )
-    right = lax.psum(part_right, ("replica", "model"))
+    right = lax.psum(lax.psum(part_right, "model"), "replica")
     gram = gram + 0.001 * jnp.mean(jnp.diagonal(gram, axis1=1, axis2=2), axis=1)[
         :, None, None
     ] * jnp.eye(RANK, dtype=jnp.float32)

time: 246 us -> 235 us (0.955)
  waiting for transfers between devices: 170 us -> 159 us
    psum x1 -> x2, waiting for transfers between devices: 111 us -> 100 us  [shards(): right = lax.psum(lax.psum(part_right, 'model'), 'replica')]
  transfers between devices with their start and end apart: 2 -> 3, of which waited for: 2 -> 3; matrix products, arithmetic and copies ran while one was open for 5% -> 5% of each run, Pallas kernels for 0% -> 0%
where the time goes in v1:
time: 235 us
  waiting for transfers between devices  159 us (68%)
  blocking collectives  29.4 us (13%)
  matrix products  16.8 us (7%)
  other arithmetic  14 us (6%)
  between operations  13.8 us (6%)
    psum x2, waiting for transfers between devices, shards(): right = lax.psum(lax.psum(part_right, 'model'), 'replica')  100 us
    reduce_scatter x1, waiting for transfers between devices, shards(): lax.psum_scatter(part_left, 'replica', scatter_dimension=1, tiled=True)  58.9 us
    all_gather x1, blocking collectives, shards(): left = lax.all_gather(shares, 'replica', axis=1, tiled=True)  21.1 us
    psum x1, blocking collectives, shards(): gram = lax.psum(part_gram, 'model')  8.32 us
    dot_general x1, matrix products, shards(): jnp.einsum('liw,lwr->lir', own_grads, last_basis.astype(jnp.bfloat16), pr...  6.75 us
    another operation x4, other arithmetic, shards(): root = jnp.linalg.cholesky(gram)  6.01 us
    dot_general x1, matrix products, shards(): jnp.einsum('liw,lir->lwr', own_grads, small_left, preferred_element_type=...  5.78 us
    another operation x3, other arithmetic, shards(): lax.linalg.triangular_solve(root, half, left_side=True, lower=True, trans...  4.99 us
  transfers between devices with their start and end apart: 3, of which 3 were waited for; matrix products, arithmetic and copies ran while one was open for 5% of the time, Pallas kernels for 0%

profile of v1, /device:TPU:0, one launch (start us, length us, event | category | flops | bytes accessed | tf_op | source)
XLA Modules:
  0.0 234.8 jit_solution(10342738010447365730)
XLA Ops:
  7.2 6.7 %fusion.2 = f32[2,2048,32]{1,2,0:T(8,128)} fusion(bf16[1,2,2048,1024]{3,2,1,0:T(8,128)(2,1)} %param.4, f32[2,1024,32]{1,2,0:T(8,128)} %param.5), kind=kOutput, calls=%fused_computation.3 | convolution fusion | flops 268500992 | bytes 9175040 | tf_op jit(solution)/shard_map/liw,lwr->lir/dot_general | solution.py:11
  14.0 0.0 all-reduce.3.cloned.1.call-start
  14.0 0.1 copy.13
  14.2 58.9 %reduce-scatter.2.cloned.1.call-done = f32[2,128,32]{1,2,0:T(8,128)} async-done(((f32[2,2048,32]{1,2,0:T(8,128)}), f32[2,128,32]{1,2,0:T(8,128)}) %reduce-scatter.2.cloned.1.call-update) | async-done | bytes 32784 | tf_op jit(solution)/shard_map/reduce_scatter | solution.py:17
  73.1 21.1 %all_gather.3 = f32[2,2048,32]{1,2,0:T(8,128)S(1)} all-gather(f32[2,128,32]{1,2,0:T(8,128)} %reduce-scatter.2.cloned.1.call-done), channel_id=1, replica_groups=mesh['replica'=16,'model'=2] {'replica'}, dimensions={1}, use_global_device_ids=true | all-gather | bytes 557056 | tf_op jit(solution)/shard_map/all_gather | solution.py:18
  94.1 0.6 fusion.18
  94.7 5.8 %fusion.5 = f32[2,1024,32]{1,2,0:T(8,128)} fusion(bf16[1,2,2048,1024]{3,2,1,0:T(8,128)(2,1)} %param.4, f32[2,2048,32]{1,2,0:T(8,128)S(1)} %all_gather.3), kind=kOutput, calls=%fused_computation.7 | convolution fusion | flops 268566528 | bytes 9175040 | tf_op jit(solution)/shard_map/liw,lir->lwr/dot_general | solution.py:22
  100.5 8.3 %psum.21 = f32[2,32,32]{1,2,0:T(8,128)S(1)} all-reduce(f32[2,32,32]{1,2,0:T(8,128)S(1)} %fusion.18), channel_id=1, replica_groups=mesh['replica'=16,'model'=2] {'model'}, use_global_device_ids=true, to_apply=%region_1.0 | all-reduce | flops 2048 | bytes 16384 | tf_op jit(solution)/shard_map/psum | solution.py:21
  108.9 0.6 copy.12
  109.5 0.7 gather_fusion
  110.2 0.1 multiply_add_fusion
  110.3 0.1 copy.14
  110.4 0.1 fusion.14
  110.4 5.9 %custom-call.9 = f32[2,32,32]{2,1,0:T(8,128)S(1)} custom-call(f32[2,32,32]{2,1,0:T(8,128)S(1)} %fusion.14), custom_call_target="Cholesky" | custom-call | tf_op jit(solution)/shard_map/jit(cholesky)/cholesky | solution.py:31
  116.3 0.1 compare_reduce_fusion
  116.4 12.2 %all-reduce.3.cloned.1.call-done = f32[2,1024,32]{1,2,0:T(8,128)} async-done(((f32[2,1024,32]{1,2,0:T(8,128)}), f32[2,1024,32]{1,2,0:T(8,128)}) %all-reduce.3.cloned.1.call-update) | async-done | bytes 262160 | tf_op jit(solution)/shard_map/psum | solution.py:25
  128.6 0.1 select_bitcast_fusion
  128.7 4.9 %custom-call.10 = f32[2,1,32,32]{2,3,1,0:T(8,128)S(1)} custom-call(f32[2,1,32,32]{3,2,1,0:T(8,128)S(1)} %select_bitcast_fusion), custom_call_target="InvertDiagBlocksLowerTriangular" | custom-call | tf_op jit(solution)/shard_map/triangular_solve | solution.py:35
  133.6 88.1 %all-reduce.5.cloned.1.call-done = f32[2,1024,32]{1,2,0:T(8,128)} async-done(((f32[2,1024,32]{1,2,0:T(8,128)}), f32[2,1024,32]{1,2,0:T(8,128)}) %all-reduce.5.cloned.1.call-update) | async-done | bytes 262160 | tf_op jit(solution)/shard_map/psum | solution.py:25
  221.8 1.1 multiply_reduce_fusion
  222.8 1.0 fusion.12
  223.9 0.2 fusion.10
  224.1 2.5 %multiply_subtract_fusion = (f32[2,2048,64]{1,2,0:T(8,128)}, f32[2,2048,64]{1,2,0:T(8,128)}) fusion(f32[2,2048,64]{1,2,0:T(8,128)S(1)} %copy-done, f32[2,2048,32]{1,2,0:T(8,128)S(1)} %all_gather.3, f32[2,32,64]{2,1,0:T(8,128)S(1)} %fusion.10, f32[2,2048,64]{1,2,0:T(8,128)S(1)} %copy-done.1), kind=kOutput, calls=%fused_computation.8 | convolution fusion | flops 101974016 | bytes 4734976 | tf_op jit(solution)/shard_map/lir,lrw->liw/dot_general | solution.py:36
  226.6 1.7 broadcast_multiply_fusion
  (17 shorter events, 0.2 us)
Async XLA Ops:
  7.2 65.9 %reduce-scatter.2.cloned.1.call-start = ((), (), s32[]{:S(2)}) async-start(), calls=%async_computation.1 | async-start | bytes 557056 | tf_op jit(solution)/shard_map/reduce_scatter | solution.py:17
  14.0 114.6 %all-reduce.3.cloned.1.call-start = ((), (), s32[]{:S(2)}) async-start(), calls=%async_computation.2 | async-start | bytes 524288 | tf_op jit(solution)/shard_map/psum | solution.py:25
  94.7 129.4 %copy-start = (f32[2,2048,64]{1,2,0:T(8,128)S(1)}, f32[2,2048,64]{1,2,0:T(8,128)}, u32[]{:S(2)}) copy-start(f32[2,2048,64]{1,2,0:T(8,128)} %param.6) | copy-start | bytes 3145732
  94.7 129.4 %copy-start.1 = (f32[2,2048,64]{1,2,0:T(8,128)S(1)}, f32[2,2048,64]{1,2,0:T(8,128)}, u32[]{:S(2)}) copy-start(f32[2,2048,64]{1,2,0:T(8,128)} %param.7) | copy-start | bytes 3145732
  108.9 112.9 %all-reduce.5.cloned.1.call-start = ((), (), s32[]{:S(2)}) async-start(), calls=%async_computation.3 | async-start | bytes 524288 | tf_op jit(solution)/shard_map/psum | solution.py:25
Sparse Core Ops, SparseCore 0:
  14.1 58.9 reduce-scatter.1
  109.0 19.5 all-reduce.2
  132.0 89.7 all-reduce.4

commit v2 on v0

--- a/solution.py
+++ b/solution.py
@@ -22,7 +22,7 @@
     part_right = jnp.einsum(
         "liw,lir->lwr", own_grads, small_left, preferred_element_type=jnp.float32
     )
-    right = lax.psum(part_right, ("replica", "model"))
+    right = jnp.sum(lax.all_gather(part_right, ("replica", "model")), axis=0)
     gram = gram + 0.001 * jnp.mean(jnp.diagonal(gram, axis1=1, axis2=2), axis=1)[
         :, None, None
     ] * jnp.eye(RANK, dtype=jnp.float32)

time: 246 us -> 189 us (0.77)
  waiting for transfers between devices: 170 us -> 112 us
    psum x1 -> x0, waiting for transfers between devices: 111 us -> none  [shards(): right = lax.psum(part_right, ('replica', 'model'))]
    all_gather x0 -> x1, waiting for transfers between devices: none -> 52.8 us  [shards(): right = jnp.sum(lax.all_gather(part_right, ('replica', 'model')), axis=0)]
    reduce_sum x0 -> x1, other arithmetic: none -> 3.98 us  [shards(): right = jnp.sum(lax.all_gather(part_right, ('replica', 'model')), axis=0)]
  transfers between devices with their start and end apart: 2 -> 2, of which waited for: 2 -> 2; matrix products, arithmetic and copies ran while one was open for 5% -> 7% of each run, Pallas kernels for 0% -> 0%
where the time goes in v2:
time: 189 us
  waiting for transfers between devices  112 us (59%)
  blocking collectives  29.5 us (16%)
  other arithmetic  16.1 us (9%)
  matrix products  15.9 us (8%)
  between operations  14.1 us (7%)
    reduce_scatter x1, waiting for transfers between devices, shards(): lax.psum_scatter(part_left, 'replica', scatter_dimension=1, tiled=True)  59 us
    all_gather x1, waiting for transfers between devices, shards(): right = jnp.sum(lax.all_gather(part_right, ('replica', 'model')), axis=0)  52.8 us
    all_gather x1, blocking collectives, shards(): left = lax.all_gather(shares, 'replica', axis=1, tiled=True)  21.1 us
    psum x1, blocking collectives, shards(): gram = lax.psum(part_gram, 'model')  8.47 us
    dot_general x1, matrix products, shards(): jnp.einsum('liw,lwr->lir', own_grads, last_basis.astype(jnp.bfloat16), pr...  6.75 us
    another operation x4, other arithmetic, shards(): root = jnp.linalg.cholesky(gram)  6.01 us
    dot_general x1, matrix products, shards(): jnp.einsum('liw,lir->lwr', own_grads, small_left, preferred_element_type=...  5.63 us
    another operation x3, other arithmetic, shards(): lax.linalg.triangular_solve(root, half, left_side=True, lower=True, trans...  5.03 us
  transfers between devices with their start and end apart: 2, of which 2 were waited for; matrix products, arithmetic and copies ran while one was open for 7% of the time, Pallas kernels for 0%

profile of v2, /device:TPU:0, one launch (start us, length us, event | category | flops | bytes accessed | tf_op | source)
XLA Modules:
  0.0 189.0 jit_solution(9224500160733540844)
XLA Ops:
  7.2 6.7 %fusion.2 = f32[2,2048,32]{1,2,0:T(8,128)} fusion(bf16[1,2,2048,1024]{3,2,1,0:T(8,128)(2,1)} %param.4, f32[2,1024,32]{1,2,0:T(8,128)} %param.5), kind=kOutput, calls=%fused_computation.3 | convolution fusion | flops 268500992 | bytes 9175040 | tf_op jit(solution)/shard_map/liw,lwr->lir/dot_general | solution.py:11
  14.0 0.0 all-gather.3.cloned.1.call-start
  14.0 59.0 %reduce-scatter.2.cloned.1.call-done = f32[2,128,32]{1,2,0:T(8,128)} async-done(((f32[2,2048,32]{1,2,0:T(8,128)}), f32[2,128,32]{1,2,0:T(8,128)}) %reduce-scatter.2.cloned.1.call-update) | async-done | bytes 32784 | tf_op jit(solution)/shard_map/reduce_scatter | solution.py:17
  73.1 21.1 %all_gather.9 = f32[2,2048,32]{1,2,0:T(8,128)S(1)} all-gather(f32[2,128,32]{1,2,0:T(8,128)} %reduce-scatter.2.cloned.1.call-done), channel_id=1, replica_groups=mesh['replica'=16,'model'=2] {'replica'}, dimensions={1}, use_global_device_ids=true | all-gather | bytes 557056 | tf_op jit(solution)/shard_map/all_gather | solution.py:18
  94.1 5.6 %fusion.5 = f32[2,1024,32]{1,2,0:T(8,128)} fusion(bf16[1,2,2048,1024]{3,2,1,0:T(8,128)(2,1)} %param.4, f32[2,2048,32]{1,2,0:T(8,128)S(1)} %all_gather.9), kind=kOutput, calls=%fused_computation.7 | convolution fusion | flops 268566528 | bytes 9175040 | tf_op jit(solution)/shard_map/liw,lir->lwr/dot_general | solution.py:22
  99.8 0.1 copy.17
  99.9 0.6 fusion.18
  100.5 8.5 %psum.7 = f32[2,32,32]{1,2,0:T(8,128)S(1)} all-reduce(f32[2,32,32]{1,2,0:T(8,128)S(1)} %fusion.18), channel_id=1, replica_groups=mesh['replica'=16,'model'=2] {'model'}, use_global_device_ids=true, to_apply=%region_1.0 | all-reduce | flops 2048 | bytes 16384 | tf_op jit(solution)/shard_map/psum | solution.py:21
  109.0 0.6 copy.16
  109.5 0.7 gather_fusion
  110.3 0.1 multiply_add_fusion
  110.3 0.1 copy.18
  110.4 0.1 fusion.14
  110.5 5.9 %custom-call.9 = f32[2,32,32]{2,1,0:T(8,128)S(1)} custom-call(f32[2,32,32]{2,1,0:T(8,128)S(1)} %fusion.14), custom_call_target="Cholesky" | custom-call | tf_op jit(solution)/shard_map/jit(cholesky)/cholesky | solution.py:31
  116.4 0.1 compare_reduce_fusion
  116.5 0.1 select_bitcast_fusion
  116.6 4.9 %custom-call.10 = f32[2,1,32,32]{2,3,1,0:T(8,128)S(1)} custom-call(f32[2,1,32,32]{3,2,1,0:T(8,128)S(1)} %select_bitcast_fusion), custom_call_target="InvertDiagBlocksLowerTriangular" | custom-call | tf_op jit(solution)/shard_map/triangular_solve | solution.py:35
  121.5 52.8 %all-gather.3.cloned.1.call-done = f32[64,1024,32]{1,2,0:T(8,128)} async-done(((f32[2,1024,32]{1,2,0:T(8,128)}), f32[64,1024,32]{1,2,0:T(8,128)}) %all-gather.3.cloned.1.call-update) | async-done | bytes 8388624 | tf_op jit(solution)/shard_map/all_gather | solution.py:25
  174.3 4.0 %reduce_sum.28 = f32[2,1024,32]{1,2,0:T(8,128)S(1)} reduce(f32[32,2,1024,32]{2,3,1,0:T(8,128)} %bitcast.28, f32[]{:T(128)} %constant.68.clone.1), dimensions={0}, to_apply=%region_5.6 | reduce | flops 2031616 | bytes 8650756 | tf_op jit(solution)/shard_map/reduce_sum | solution.py:25
  178.3 0.1 multiply_reduce_fusion
  178.4 0.3 fusion.12
  178.7 0.2 fusion.10
  178.9 0.8 broadcast_multiply_fusion
  179.6 2.5 %multiply_subtract_fusion = (f32[2,2048,64]{1,2,0:T(8,128)}, f32[2,2048,64]{1,2,0:T(8,128)}) fusion(f32[2,2048,64]{1,2,0:T(8,128)S(1)} %copy-done, f32[2,2048,32]{1,2,0:T(8,128)S(1)} %all_gather.9, f32[2,32,64]{2,1,0:T(8,128)S(1)} %fusion.10, f32[2,2048,64]{1,2,0:T(8,128)S(1)} %copy-done.1), kind=kOutput, calls=%fused_computation.8 | convolution fusion | flops 101974016 | bytes 4734976 | tf_op jit(solution)/shard_map/lir,lrw->liw/dot_general | solution.py:36
  (15 shorter events, 0.2 us)
Async XLA Ops:
  7.2 65.9 %reduce-scatter.2.cloned.1.call-start = ((), (), s32[]{:S(2)}) async-start(), calls=%async_computation.1 | async-start | bytes 557056 | tf_op jit(solution)/shard_map/reduce_scatter | solution.py:17
  14.0 160.3 %all-gather.3.cloned.1.call-start = ((), (), s32[]{:S(2)}) async-start(), calls=%async_computation.2 | async-start | bytes 8650752 | tf_op jit(solution)/shard_map/all_gather | solution.py:25
  99.8 79.9 %copy-start = (f32[2,2048,64]{1,2,0:T(8,128)S(1)}, f32[2,2048,64]{1,2,0:T(8,128)}, u32[]{:S(2)}) copy-start(f32[2,2048,64]{1,2,0:T(8,128)} %param.6) | copy-start | bytes 3145732
  99.8 79.9 %copy-start.1 = (f32[2,2048,64]{1,2,0:T(8,128)S(1)}, f32[2,2048,64]{1,2,0:T(8,128)}, u32[]{:S(2)}) copy-start(f32[2,2048,64]{1,2,0:T(8,128)} %param.7) | copy-start | bytes 3145732
Sparse Core Ops, SparseCore 0:
  14.1 58.9 reduce-scatter.1
  99.9 74.3 all-gather.2
